TPU v7x, 32 devices: a whole 2x2x4 slice. The times are simulated.
32 devices in a mesh: row: 2 (over y), col: 4 (over z), layer: 4 (over x, core).
Axes of the slice: x: 2, y: 2, z: 4, core: 2. Of those that a mesh axis runs over, the one named last changes fastest.
Arguments:
- density_tiles: bfloat16 [192, 4, 2, 128, 128], P(('row', 'col')), may hold values from -1.5 to 1.5
- tile_columns: int32 [192, 4, 2], P(('row', 'col')), may hold values from -1 to 191, as said below
Outputs:
- square_tiles: bfloat16 [192, 4, 2, 128, 128], P(('row', 'col'), None, None, 'layer')
Inputs may be any that keep to these rules, and one draw needn't show every extreme that they name: `tile_columns`: entry [i, g, s] is a tile column in group g (columns g * 48 to (g + 1) * 48 - 1) or -1; within one block row and group the listed columns are distinct and empty slots come after the listed ones; block row i lists its own column i in the first slot of its group, whose 2 slots are all listed; other groups hold 0 to 2 listed tiles.
All inputs are finite; a program needn't handle non-finite values.
Results may differ from a plain program's by a relative error of at most 0.0048.
Values may be sent and summed in bfloat16 or wider, within the bound.
A program may use at most 128 MiB of HBM per device.

v0:
```python
import jax
import jax.numpy as jnp
from jax import lax
from jax.sharding import PartitionSpec as P


def spread(value, axis, source):
    kept = jnp.where(lax.axis_index(axis) == source, value, 0).astype(value.dtype)
    return lax.psum(kept, axis)


def multiply(left_tiles, left_columns, right_tiles, right_columns, target_columns, start_row):
    is_live = left_columns >= 0
    inner_rows = jnp.where(is_live, left_columns - start_row, 0).astype(jnp.int32)
    inner_columns = right_columns[inner_rows]
    matches = (
        (inner_columns[:, :, None, :] == target_columns[:, None, :, None])
        & is_live[:, :, None, None]
        & (target_columns >= 0)[:, None, :, None]
    )
    slot_index = jnp.argmax(matches.astype(jnp.int32), axis=-1)
    located = jnp.any(matches, axis=-1)
    selected = right_tiles[inner_rows[:, :, None], slot_index]
    selected = jnp.where(located[:, :, :, None, None], selected, jnp.zeros((), jnp.bfloat16))
    return jnp.einsum("iarc,iascd->isrd", left_tiles, selected, preferred_element_type=jnp.float32)


def on_device(density_tiles, tile_columns):
    row_count = lax.axis_size("row")
    column_count = lax.axis_size("col")
    layer_count = lax.axis_size("layer")
    grid_tiles, grid_columns = (
        lax.all_to_all(density_tiles, "col", split_axis=1, concat_axis=0, tiled=True),
        lax.all_to_all(tile_columns, "col", split_axis=1, concat_axis=0, tiled=True),
    )
    block_tiles = grid_tiles[:, 0]
    block_columns = grid_columns[:, 0]
    group_rows = block_tiles.shape[0]
    row_ratio = column_count // row_count
    panel_rows = group_rows // row_ratio
    per_layer = column_count // layer_count
    layer_index = lax.axis_index("layer")
    partial_value = jnp.zeros(block_tiles.shape, jnp.float32)
    for panel_step in range(per_layer):
        panel_index = layer_index * per_layer + panel_step
        left_tiles, left_columns = (
            spread(block_tiles, "col", panel_index),
            spread(block_columns, "col", panel_index),
        )
        offset = panel_index % row_ratio * panel_rows
        part_tiles = lax.dynamic_slice_in_dim(block_tiles, offset, panel_rows, 0)
        part_columns = lax.dynamic_slice_in_dim(block_columns, offset, panel_rows, 0)
        right_tiles, right_columns = (
            spread(part_tiles, "row", panel_index // row_ratio),
            spread(part_columns, "row", panel_index // row_ratio),
        )
        partial_value = partial_value + multiply(
            left_tiles,
            left_columns,
            right_tiles,
            right_columns,
            block_columns,
            panel_index * panel_rows,
        )
    rounded = partial_value.astype(jnp.bfloat16)
    summed = lax.psum_scatter(
        rounded.astype(jnp.float32).astype(jnp.bfloat16), "layer", scatter_dimension=2, tiled=True
    )
    returned = lax.all_to_all(summed[:, None], "col", split_axis=0, concat_axis=1, tiled=True)
    return returned


def solution(mesh):
    in_specs = (P(("row", "col"), None, None, None, None), P(("row", "col"), None, None))
    out_specs = P(("row", "col"), None, None, "layer", None)
    return jax.shard_map(
        on_device, mesh=mesh, in_specs=in_specs, out_specs=out_specs, check_vma=False
    )
```

profile of v0, /device:TPU:0, one launch (start us, length us, event | category | flops | bytes accessed | tf_op | source)
XLA Modules:
  0.0 603.0 jit_solution(9816034779347705298)
XLA Ops:
  6.5 8.1 %copy.33 = bf16[24,4,2,128,128]{4,3,2,0,1:T(8,128)(2,1)} copy(bf16[24,4,2,128,128]{4,3,2,1,0:T(8,128)(2,1)} %param.2) | data formatting | bytes 12582912 | tf_op args[0]
  14.6 6.3 %all-to-all-start.1 = ((bf16[24,4,2,128,128]{4,3,2,0,1:T(8,128)(2,1)}), bf16[24,4,2,128,128]{4,3,2,0,1:T(8,128)(2,1)}, u32[]{:S(2)}, u32[]{:S(2)}) async-start(bf16[24,4,2,128,128]{4,3,2,0,1:T(8,128)(2,1)} %copy.33), calls=%async_computation.1 | async-start | bytes 12582912 | tf_op jit(solution)/shard_map/all_to_all | solution.py:33
  21.0 138.7 %all-to-all-done.1 = bf16[24,4,2,128,128]{4,3,2,0,1:T(8,128)(2,1)} async-done(((bf16[24,4,2,128,128]{4,3,2,0,1:T(8,128)(2,1)}), bf16[24,4,2,128,128]{4,3,2,0,1:T(8,128)(2,1)}, u32[]{:S(2)}, u32[]{:S(2)}) %all-to-all-start.1) | async-done | bytes 6291488 | tf_op jit(solution)/shard_map/all_to_all | solution.py:33
  159.7 3.7 dynamic-slice_select_fusion
  163.5 6.3 %broadcast_select_fusion = bf16[96,2,128,128]{3,2,1,0:T(8,128)(2,1)} fusion(pred[]{:T(512)S(6)} %eq.26, bf16[24,4,2,128,128]{4,3,2,0,1:T(8,128)(2,1)} %all-to-all-done.1), kind=kLoop, calls=%fused_computation.9 | loop fusion | flops 3145728 | bytes 12582913 | tf_op jit(solution)/shard_map/jit(_where)/select_n | solution.py:8
  169.9 3.3 all-to-all-start
  173.1 0.0 reduce-scatter.2.cloned.1.call-start
  173.2 5.5 all-to-all-done
  178.7 0.1 copy.27
  178.8 0.1 copy.31
  178.9 16.6 %psum.29 = s32[96,2]{1,0:T(8,128)S(1)} all-reduce(s32[96,2]{1,0:T(8,128)S(1)} %broadcast_select_fusion.1), channel_id=1, replica_groups=mesh['row'=2,'col'=4,'layer'=4] {'col'}, use_global_device_ids=true, to_apply=%region_1.2 | all-reduce | flops 192 | bytes 1536 | tf_op jit(solution)/shard_map/psum | solution.py:9
  195.6 0.1 copy.30
  195.6 0.1 copy.29
  195.8 0.1 reshape.19
  195.9 8.8 %psum.28 = s32[48,2]{1,0:T(8,128)S(1)} all-reduce(s32[48,2]{1,0:T(8,128)S(1)} %dynamic-slice_select_fusion.1), channel_id=1, replica_groups=mesh['row'=2,'col'=4,'layer'=4] {'row'}, use_global_device_ids=true, to_apply=%region_0.1 | all-reduce | flops 96 | bytes 768 | tf_op jit(solution)/shard_map/psum | solution.py:9
  204.7 0.7 gather_fusion
  205.4 0.1 copy.28
  205.5 0.1 copy.34
  205.6 0.6 iota_reduce_fusion
  206.2 0.1 copy.35
  206.4 0.2 reshape.25
  206.5 0.2 copy.32
  206.7 42.4 %all-reduce.3.cloned.1.call-done = bf16[48,2,128,128]{3,2,1,0:T(8,128)(2,1)} async-done(((bf16[48,2,128,128]{3,2,1,0:T(8,128)(2,1)}), bf16[48,2,128,128]{3,2,1,0:T(8,128)(2,1)}) %all-reduce.3.cloned.1.call-update) | async-done | bytes 3145744 | tf_op jit(solution)/shard_map/psum | solution.py:9
  249.1 18.2 %gather_fusion.1 = bf16[384,128,128]{2,1,0:T(8,128)(2,1)} fusion(bf16[48,2,128,128]{3,2,1,0:T(8,128)(2,1)} %all-reduce.3.cloned.1.call-done, s32[384]{0:T(512)S(1)} %reshape.25), kind=kCustom, calls=%fused_computation.1 | custom fusion | bytes 25168896 | tf_op jit(solution)/shard_map/gather | solution.py:23
  267.3 16.6 %copy.36 = bf16[96,2,2,128,128]{3,4,1,2,0:T(8,128)(2,1)} copy(bf16[96,2,2,128,128]{4,3,2,1,0:T(8,128)(2,1)} %bitcast.41) | data formatting | bytes 25165824 | tf_op jit(solution)/shard_map/gather | solution.py:23
  284.0 190.4 %all-reduce.5.cloned.1.call-done = bf16[96,2,128,128]{3,2,1,0:T(8,128)(2,1)} async-done(((bf16[96,2,128,128]{3,2,1,0:T(8,128)(2,1)}), bf16[96,2,128,128]{3,2,1,0:T(8,128)(2,1)}) %all-reduce.5.cloned.1.call-update) | async-done | bytes 6291472 | tf_op jit(solution)/shard_map/psum | solution.py:9
  474.4 10.0 %fusion.3 = bf16[96,2,128,128]{2,3,1,0:T(8,128)(2,1)} fusion(bf16[96,2,128,128]{3,2,1,0:T(8,128)(2,1)} %all-reduce.5.cloned.1.call-done, bf16[96,2,2,128,128]{3,4,1,2,0:T(8,128)(2,1)} %copy.36, pred[96,2,2]{1,2,0:T(4,128)(4,1)S(1)} %copy.32), kind=kOutput, calls=%fused_computation.6 | convolution fusion | flops 1620049920 | bytes 25166208 | tf_op jit(solution)/shard_map/iarc,iascd->isrd/dot_general | solution.py:25
  484.4 9.1 %copy.37 = bf16[96,2,128,128]{3,0,1,2:T(8,128)(2,1)} copy(bf16[96,2,128,128]{2,3,1,0:T(8,128)(2,1)} %fusion.3) | data formatting | bytes 12582912 | tf_op jit(solution)/shard_map/convert_element_type | solution.py:65
  493.5 57.9 %reduce-scatter.2.cloned.1.call-done = bf16[96,2,32,128]{3,0,1,2:T(8,128)(2,1)} async-done(((bf16[96,2,128,128]{3,0,1,2:T(8,128)(2,1)}), bf16[96,2,32,128]{3,0,1,2:T(8,128)(2,1)}) %reduce-scatter.2.cloned.1.call-update) | async-done | bytes 1572880 | tf_op jit(solution)/shard_map/reduce_scatter | solution.py:66
  551.4 2.4 copy.38
  553.8 41.2 %all_to_all.48 = bf16[96,1,2,32,128]{4,3,2,1,0:T(8,128)(2,1)S(1)} all-to-all(bf16[96,1,2,32,128]{4,3,2,1,0:T(8,128)(2,1)S(1)} %copy.38), channel_id=1, replica_groups=mesh['row'=2,'col'=4,'layer'=4] {'col'}, dimensions={0} | all-to-all | bytes 3145728 | tf_op jit(solution)/shard_map/all_to_all | solution.py:69
  595.0 1.4 copy.43
  (13 shorter events, 0.2 us)
Async XLA Ops:
  14.6 145.1 %all-to-all-start.1 = ((bf16[24,4,2,128,128]{4,3,2,0,1:T(8,128)(2,1)}), bf16[24,4,2,128,128]{4,3,2,0,1:T(8,128)(2,1)}, u32[]{:S(2)}, u32[]{:S(2)}) async-start(bf16[24,4,2,128,128]{4,3,2,0,1:T(8,128)(2,1)} %copy.33), calls=%async_computation.1 | async-start | bytes 12582912 | tf_op jit(solution)/shard_map/all_to_all | solution.py:33
  21.0 228.1 %all-reduce.3.cloned.1.call-start = ((), (), s32[]{:S(2)}) async-start(), calls=%async_computation.4 | async-start | bytes 6291456 | tf_op jit(solution)/shard_map/psum | solution.py:9
  163.4 310.9 %all-reduce.5.cloned.1.call-start = ((), (), s32[]{:S(2)}) async-start(), calls=%async_computation.5 | async-start | bytes 12582912 | tf_op jit(solution)/shard_map/psum | solution.py:9
  169.9 8.8 %all-to-all-start = ((s32[24,4,2]{0,2,1:T(2,128)}), s32[24,4,2]{0,2,1:T(2,128)S(1)}, u32[]{:S(2)}, u32[]{:S(2)}) async-start(s32[24,4,2]{0,2,1:T(2,128)} %param.3), calls=%async_computation | async-start | bytes 8192 | tf_op jit(solution)/shard_map/all_to_all | solution.py:34
  173.1 378.3 %reduce-scatter.2.cloned.1.call-start = ((), (), s32[]{:S(2)}) async-start(), calls=%async_computation.6 | async-start | bytes 7864320 | tf_op jit(solution)/shard_map/reduce_scatter | solution.py:66
Sparse Core Ops, SparseCore 0:
  163.6 85.4 all-reduce.2
  251.5 222.8 all-reduce.4
  493.6 57.7 reduce-scatter.1
where the time goes:
time: 604 us; the launch traced here: 603 us
  waiting for transfers between devices  435 us (72%)
  blocking collectives  66.6 us (11%)
  local copies, waits for them, and re-layouts  57.7 us (10%)
  between operations  13.2 us (2%)
  other arithmetic  10.8 us (2%)
  matrix products  10 us (2%)
  starting transfers between devices  9.69 us (2%)
    psum x2, waiting for transfers between devices, spread(): return lax.psum(kept, axis)  233 us
    all_to_all x1, waiting for transfers between devices, on_device(): lax.all_to_all(density_tiles, 'col', split_axis=1, concat_axis=0, tiled=T...  139 us
    reduce_scatter x1, waiting for transfers between devices, on_device(): lax.psum_scatter(rounded.astype(jnp.float32).astype(jnp.bfloat16), 'layer...  57.9 us
    all_to_all x1, blocking collectives, on_device(): lax.all_to_all(summed[:, None], 'col', split_axis=0, concat_axis=1, tiled...  41.2 us
    gather x2, local copies, waits for them, and re-layouts, multiply(): selected = right_tiles[inner_rows[:, :, None], slot_index]  34.9 us
    psum x2, blocking collectives, spread(): return lax.psum(kept, axis)  25.4 us
  transfers between devices with their start and end apart: 5, of which 5 were waited for; matrix products, arithmetic and copies ran while one was open for 7% of the time, Pallas kernels for 0%

commit v1 on v0

v1 whole, which is shorter than its diff:
```python
import functools

import jax
import jax.numpy as jnp
from jax import lax
from jax.experimental import pallas as pl
from jax.experimental.pallas import tpu as pltpu
from jax.sharding import PartitionSpec as P

MESH = pl.DeviceIdType.MESH


def divisor(total, most):
    return max(d for d in range(1, most + 1) if total % d == 0)


def kernel(
    sizes, columns_ref, tiles_ref, meta_ref, out_ref,
    left, right, meta_all, meta_smem, stage,
    local_sem, meta_send, meta_recv, send_sem, recv_sem, out_send, out_recv,
):
    row_count, col_count, layer_count, chunks, out_chunks, is_balanced = sizes
    n, group_count, slots, tile, _ = tiles_ref.shape
    cells = row_count * col_count
    per_layer = group_count // layer_count
    quarter = tile // layer_count
    width = group_count * slots
    r, c, l = lax.axis_index("row"), lax.axis_index("col"), lax.axis_index("layer")
    me = r * col_count + c
    own_groups = pl.ds(l * per_layer, per_layer)

    own_copy = pltpu.make_async_copy(
        tiles_ref.at[:, own_groups], right.at[pl.ds(me * n, n)], local_sem.at[0]
    )
    left_copy = pltpu.make_async_copy(tiles_ref, left, local_sem.at[1])
    meta_copy = pltpu.make_async_copy(meta_ref, meta_all.at[pl.ds(me * n, n)], local_sem.at[2])
    own_copy.start()
    meta_copy.start()
    left_copy.start()
    right[cells * n] = jnp.zeros(right.shape[1:], right.dtype)

    def cell_id(offset):
        target = lax.rem(me + offset, cells)
        return {"row": lax.div(target, col_count), "col": lax.rem(target, col_count)}

    def layer_id(offset):
        return {"layer": lax.rem(l + offset, layer_count)}

    barrier = pltpu.get_barrier_semaphore()
    for offset in range(1, cells):
        pl.semaphore_signal(barrier, inc=1, device_id=cell_id(offset), device_id_type=MESH)
    for offset in range(1, layer_count):
        pl.semaphore_signal(barrier, inc=1, device_id=layer_id(offset), device_id_type=MESH)
    pl.semaphore_wait(barrier, cells - 1 + layer_count - 1)
    own_copy.wait()

    step_rows = n // chunks
    sent = []

    def rows_of(cell, chunk):
        return pl.ds(cell * n + chunk * step_rows, step_rows)

    def copy_of(cell, chunk, way, device):
        return pltpu.make_async_remote_copy(
            src_ref=right.at[rows_of(cell, chunk)],
            dst_ref=right.at[rows_of(cell, chunk)],
            send_sem=send_sem.at[way, cell, chunk],
            recv_sem=recv_sem.at[cell, chunk],
            device_id=device,
            device_id_type=MESH,
        )

    ways = {
        "up": (0, c < col_count - 1, {"col": jnp.minimum(c + 1, col_count - 1)}),
        "down": (1, c > 0, {"col": jnp.maximum(c - 1, 0)}),
        "south": (2, r < row_count - 1, {"row": jnp.minimum(r + 1, row_count - 1)}),
        "north": (3, r > 0, {"row": jnp.maximum(r - 1, 0)}),
    }

    def send(cell, chunk, way, condition=True):
        index, exists, device = ways[way]
        wanted = jnp.logical_and(exists, condition)

        @pl.when(wanted)
        def _():
            copy_of(cell, chunk, index, device).start()

        sent.append((wanted, cell, chunk, index, device))

    def await_arrival(cell, chunk):
        copy_of(cell, chunk, 0, {"col": c}).wait_recv()

    for chunk in range(chunks):
        for way in ("up", "down", "south", "north"):
            send(me, chunk, way)

    meta_copy.wait()
    meta_copies = []
    for offset in range(1, cells):
        copy = pltpu.make_async_remote_copy(
            src_ref=meta_ref,
            dst_ref=meta_all.at[pl.ds(me * n, n)],
            send_sem=meta_send.at[offset],
            recv_sem=meta_recv.at[offset],
            device_id=cell_id(offset),
            device_id_type=MESH,
        )
        copy.start()
        meta_copies.append(copy)

    even = lax.rem(c, 2) == 0
    for step in range(1, col_count):
        for chunk in range(chunks):
            for origin, has, way, is_pair in (
                (c - step, c >= step, "up", jnp.logical_not(even)),
                (c + step, c + step < col_count, "down", even),
            ):
                origin = jnp.clip(origin, 0, col_count - 1)
                cell = r * col_count + origin

                @pl.when(has)
                def _():
                    await_arrival(cell, chunk)

                send(cell, chunk, way, has)
                across = has
                if is_balanced and step == 1 and chunk >= chunks // 2:
                    across = jnp.logical_and(has, jnp.logical_not(is_pair))
                send(cell, chunk, "south", across)
                send(cell, chunk, "north", across)

    if is_balanced:
        other = (1 - r) * col_count + c
        for chunk in range(chunks):
            await_arrival(other, chunk)
            if chunk >= chunks // 2:
                send(other, chunk, "up", even)
                send(other, chunk, "down", jnp.logical_not(even))
        for step in range(1, col_count):
            origin = (1 - r) * col_count + lax.rem(c + step, col_count)
            for chunk in range(chunks):
                await_arrival(origin, chunk)
    else:
        for step in range(1, row_count):
            for shift in range(col_count):
                for chunk in range(chunks):
                    for origin, has, way in (
                        (r - step, r >= step, "south"),
                        (r + step, r + step < row_count, "north"),
                    ):
                        origin = jnp.clip(origin, 0, row_count - 1)
                        cell = origin * col_count + lax.rem(c + shift, col_count)

                        @pl.when(has)
                        def _():
                            await_arrival(cell, chunk)

                        send(cell, chunk, way, has)

    for copy in meta_copies:
        copy.wait()
    table_copy = pltpu.make_async_copy(meta_all, meta_smem, local_sem.at[3])
    table_copy.start()
    table_copy.wait()
    left_copy.wait()

    def one_row(i, carry):
        targets = [
            columns_ref[i * width + l * per_layer * slots + s] for s in range(per_layer * slots)
        ]
        strips = []
        for a in range(width):
            k = columns_ref[i * width + a]
            inner = jnp.maximum(k, 0)
            pieces = []
            for s in range(per_layer * slots):
                group = s // slots
                row_index = jnp.int32(cells * n)
                slot_index = jnp.int32(0)
                is_live = (k >= 0) & (targets[s] >= 0)
                for t in range(slots):
                    hit = (meta_smem[inner, 0, group * slots + t] == targets[s]) & is_live
                    row_index = jnp.where(hit, inner, row_index)
                    slot_index = jnp.where(hit, t, slot_index)
                pieces.append(right[row_index, group, slot_index])
            strips.append(jnp.concatenate(pieces, axis=1))
        rights = jnp.concatenate(strips, axis=0)
        lefts = jnp.concatenate(
            [left[i, a // slots, a % slots] for a in range(width)], axis=1
        )
        total = jnp.dot(lefts, rights, preferred_element_type=jnp.float32).astype(stage.dtype)
        for q in range(layer_count):
            for s in range(per_layer * slots):
                stage[q, i, s // slots, s % slots] = total[
                    q * quarter:(q + 1) * quarter, s * tile:(s + 1) * tile
                ]
        return carry

    out_rows = n // out_chunks

    def out_copies(chunk):
        rows = pl.ds(chunk * out_rows, out_rows)
        copies = []
        for offset in range(layer_count):
            q = lax.rem(l + offset, layer_count)
            if offset == 0:
                copies.append(pltpu.make_async_copy(
                    stage.at[q, rows], out_ref.at[rows, own_groups], out_send.at[0, chunk]
                ))
            else:
                copies.append(pltpu.make_async_remote_copy(
                    src_ref=stage.at[q, rows],
                    dst_ref=out_ref.at[rows, own_groups],
                    send_sem=out_send.at[offset, chunk],
                    recv_sem=out_recv.at[offset, chunk],
                    device_id=layer_id(offset),
                    device_id_type=MESH,
                ))
        return copies

    all_out = []
    for chunk in range(out_chunks + 1):
        if chunk < out_chunks:
            lax.fori_loop(chunk * out_rows, (chunk + 1) * out_rows, one_row, 0)
        if chunk > 0:
            copies = out_copies(chunk - 1)
            for copy in copies[1:] + copies[:1]:
                copy.start()
            all_out.extend(copies)

    for wanted, cell, chunk, index, device in sent:
        @pl.when(wanted)
        def _():
            copy_of(cell, chunk, index, device).wait_send()

    for copy in all_out:
        copy.wait()


def on_device(density_tiles, tile_columns):
    row_count = lax.axis_size("row")
    col_count = lax.axis_size("col")
    layer_count = lax.axis_size("layer")
    n, group_count, slots, tile, _ = density_tiles.shape
    cells = row_count * col_count
    per_layer = group_count // layer_count
    quarter = tile // layer_count
    kept = per_layer * slots
    chunks = divisor(n, 4)
    out_chunks = divisor(n, 4)
    is_balanced = row_count == 2 and col_count % 2 == 0 and chunks % 2 == 0
    own = lax.dynamic_slice_in_dim(tile_columns, lax.axis_index("layer") * per_layer, per_layer, 1)
    meta = jnp.pad(own.reshape(n, 1, kept), ((0, 0), (0, 0), (0, 128 - kept)), constant_values=-1)
    dtype = density_tiles.dtype
    sizes = (row_count, col_count, layer_count, chunks, out_chunks, is_balanced)
    return pl.pallas_call(
        functools.partial(kernel, sizes),
        out_shape=jax.ShapeDtypeStruct((n, group_count, slots, quarter, tile), dtype),
        in_specs=[
            pl.BlockSpec(memory_space=pltpu.SMEM),
            pl.BlockSpec(memory_space=pl.ANY),
            pl.BlockSpec(memory_space=pltpu.VMEM),
        ],
        out_specs=pl.BlockSpec(memory_space=pl.ANY),
        scratch_shapes=[
            pltpu.VMEM(density_tiles.shape, dtype),
            pltpu.VMEM((cells * n + 1, per_layer, slots, tile, tile), dtype),
            pltpu.VMEM((cells * n, 1, 128), jnp.int32),
            pltpu.SMEM((cells * n, 1, 128), jnp.int32),
            pltpu.VMEM((layer_count, n, per_layer, slots, quarter, tile), dtype),
            pltpu.SemaphoreType.DMA((4,)),
            pltpu.SemaphoreType.DMA((cells,)),
            pltpu.SemaphoreType.DMA((cells,)),
            pltpu.SemaphoreType.DMA((4, cells, chunks)),
            pltpu.SemaphoreType.DMA((cells, chunks)),
            pltpu.SemaphoreType.DMA((layer_count, out_chunks)),
            pltpu.SemaphoreType.DMA((layer_count, out_chunks)),
        ],
        compiler_params=pltpu.CompilerParams(
            collective_id=0, has_side_effects=True, vmem_limit_bytes=60 * 1024 * 1024
        ),
    )(tile_columns.reshape(-1), density_tiles, meta)


def solution(mesh):
    in_specs = (P(("row", "col"), None, None, None, None), P(("row", "col"), None, None))
    out_specs = P(("row", "col"), None, None, "layer", None)
    return jax.shard_map(
        on_device, mesh=mesh, in_specs=in_specs, out_specs=out_specs, check_vma=False
    )
```

time: 604 us -> 158 us (0.26)
  waiting for transfers between devices: 435 us -> 0 us
  Pallas kernels: 0 us -> 152 us
  blocking collectives: 66.6 us -> 0 us
  local copies, waits for them, and re-layouts: 57.7 us -> 5.12 us
  between operations: 13.2 us -> 0.01 us
  other arithmetic: 10.8 us -> 0 us
  matrix products: 10 us -> 0 us
  starting transfers between devices: 9.69 us -> 0 us
    psum x2 -> x0, waiting for transfers between devices: 233 us -> none  [spread(): return lax.psum(kept, axis)]
    pallas_call x0 -> x1, Pallas kernels: none -> 152 us  [on_device(): pl.pallas_call(functools.partial(kernel, sizes), out_shape=jax.ShapeDtype...]
    all_to_all x2 -> x0, waiting for transfers between devices: 144 us -> none  [the longest x1 139 us: on_device(): lax.all_to_all(density_tiles, 'col', split_axis=1, concat_axis=0, tiled=T...]
    reduce_scatter x1 -> x0, waiting for transfers between devices: 57.9 us -> none  [on_device(): lax.psum_scatter(rounded.astype(jnp.float32).astype(jnp.bfloat16), 'layer...]
    all_to_all x1 -> x0, blocking collectives: 41.2 us -> none  [on_device(): lax.all_to_all(summed[:, None], 'col', split_axis=0, concat_axis=1, tiled...]
    gather x4 -> x0, local copies, waits for them, and re-layouts: 35.6 us -> none  [the longest x2 34.9 us: multiply(): selected = right_tiles[inner_rows[:, :, None], slot_index]]
    psum x2 -> x0, blocking collectives: 25.4 us -> none  [spread(): return lax.psum(kept, axis)]
    select_n x4 -> x0, other arithmetic: 10.1 us -> none  [spread(): jnp.where(lax.axis_index(axis) == source, value, 0).astype(value.dtype)]
  transfers between devices with their start and end apart: 5 -> 0, of which waited for: 5 -> 0; matrix products, arithmetic and copies ran while one was open for 7% -> 0% of each run, Pallas kernels for 0% -> 0%
where the time goes in v1:
time: 158 us; the launch traced here: 157 us
  Pallas kernels  152 us (96%)
  local copies, waits for them, and re-layouts  5.12 us (3%)
    pallas_call x1, Pallas kernels, on_device(): pl.pallas_call(functools.partial(kernel, sizes), out_shape=jax.ShapeDtype...  152 us
    unnamed x2, local copies, waits for them, and re-layouts  3.78 us

profile of v1, /device:TPU:0, one launch (start us, length us, event | category | flops | bytes accessed | tf_op | source)
XLA Modules:
  0.0 157.2 jit_solution(10071028052448389658)
XLA Ops:
  0.0 0.8 copy.4
  0.8 0.7 reshape.3.columns_ref
  1.5 0.6 pad.4.meta_ref
  2.1 152.0 %shard_map.28 = bf16[24,4,2,32,128]{4,3,2,1,0:T(8,128)(2,1)} custom-call(s32[192]{0:T(256)} %reshape.3.columns_ref, bf16[24,4,2,128,128]{4,3,2,1,0:T(8,128)(2,1)} %tiles_ref.1, s32[24,1,128]{2,1,0:T(1,128)} %pad.4.meta_ref), custom_call_target="tpu_custom_call" | custom-call | tf_op jit(solution)/shard_map/pallas_call | solution.py:256
  154.2 3.0 %copy.7 = bf16[24,4,2,32,128]{4,3,2,1,0:T(8,128)(2,1)} copy(bf16[24,4,2,32,128]{4,3,2,1,0:T(8,128)(2,1)} %shard_map.28) | data formatting | bytes 3145728
  (1 shorter events, 0.0 us)

commit v2 on v1

--- a/solution.py
+++ b/solution.py
@@ -282,9 +282,310 @@
     )(tile_columns.reshape(-1), density_tiles, meta)
 
 
+def paired_kernel(
+    sizes, tiles_ref, meta_ref, out_ref,
+    left, right, meta_all, meta_smem, stage,
+    local_sem, meta_send, meta_recv, send_sem, recv_sem, left_send, left_recv, out_send, out_recv,
+):
+    col_count, layer_count, chunks, out_chunks = sizes
+    n, group_count, slots, tile, _ = tiles_ref.shape
+    cells = 2 * col_count
+    per_layer = group_count // layer_count
+    quarter = tile // layer_count
+    width = group_count * slots
+    r, c, l = lax.axis_index("row"), lax.axis_index("col"), lax.axis_index("layer")
+    high, k = lax.div(l, 2), lax.rem(l, 2)
+    me = r * col_count + c
+    base = k * col_count + c
+    is_home = k == r
+    is_guest = jnp.logical_not(is_home)
+    group = 2 * high + r
+    own_groups = pl.ds(group * per_layer, per_layer)
+    other_groups = pl.ds((2 * high + 1 - r) * per_layer, per_layer)
+    facing = {"row": 1 - r}
+    partner = {"layer": 2 * high + 1 - k}
+
+    own_copy = pltpu.make_async_copy(
+        tiles_ref.at[:, own_groups], right.at[pl.ds(me * n, n)], local_sem.at[0]
+    )
+    left_copy = pltpu.make_async_copy(tiles_ref, left, local_sem.at[1])
+    meta_copy = pltpu.make_async_copy(meta_ref, meta_all.at[pl.ds(me * n, n)], local_sem.at[2])
+    own_copy.start()
+    meta_copy.start()
+
+    @pl.when(is_home)
+    def _():
+        left_copy.start()
+
+    right[cells * n] = jnp.zeros(right.shape[1:], right.dtype)
+
+    def cell_id(offset):
+        target = lax.rem(me + offset, cells)
+        return {"row": lax.div(target, col_count), "col": lax.rem(target, col_count)}
+
+    barrier = pltpu.get_barrier_semaphore()
+    for offset in range(1, cells):
+        pl.semaphore_signal(barrier, inc=1, device_id=cell_id(offset), device_id_type=MESH)
+    for offset in range(1, layer_count):
+        for row in (r, 1 - r):
+            pl.semaphore_signal(
+                barrier,
+                inc=1,
+                device_id={"row": row, "layer": lax.rem(l + offset, layer_count)},
+                device_id_type=MESH,
+            )
+    pl.semaphore_wait(barrier, cells - 1 + 2 * (layer_count - 1))
+
+    step_rows = n // chunks
+    sent = []
+
+    def rows_of(cell, chunk):
+        return pl.ds(cell * n + chunk * step_rows, step_rows)
+
+    def copy_of(cell, chunk, way, device):
+        source = right.at[rows_of(cell, chunk)]
+        if way == 3:
+            source = tiles_ref.at[pl.ds(chunk * step_rows, step_rows), other_groups]
+        return pltpu.make_async_remote_copy(
+            src_ref=source,
+            dst_ref=right.at[rows_of(cell, chunk)],
+            send_sem=send_sem.at[way, cell, chunk],
+            recv_sem=recv_sem.at[cell, chunk],
+            device_id=device,
+            device_id_type=MESH,
+        )
+
+    ways = {
+        "up": (0, c < col_count - 1, {"col": jnp.minimum(c + 1, col_count - 1)}),
+        "down": (1, c > 0, {"col": jnp.maximum(c - 1, 0)}),
+        "partner": (2, True, partner),
+        "facing": (3, True, facing),
+    }
+
+    def send(cell, chunk, way, condition):
+        index, exists, device = ways[way]
+        wanted = jnp.logical_and(exists, condition)
+
+        @pl.when(wanted)
+        def _():
+            copy_of(cell, chunk, index, device).start()
+
+        sent.append((wanted, cell, chunk, index, device))
+
+    def await_arrival(cell, chunk, condition):
+        @pl.when(condition)
+        def _():
+            copy_of(cell, chunk, 2, partner).wait_recv()
+
+    for chunk in range(chunks):
+        send(me, chunk, "facing", is_home)
+    own_copy.wait()
+    for chunk in range(chunks):
+        for way in ("up", "down"):
+            send(me, chunk, way, is_home)
+    left_out = pltpu.make_async_remote_copy(
+        src_ref=tiles_ref, dst_ref=left, send_sem=left_send, recv_sem=left_recv,
+        device_id=facing, device_id_type=MESH,
+    )
+
+    meta_copy.wait()
+    meta_copies = []
+    for offset in range(1, cells):
+        copy = pltpu.make_async_remote_copy(
+            src_ref=meta_ref,
+            dst_ref=meta_all.at[pl.ds(me * n, n)],
+            send_sem=meta_send.at[offset],
+            recv_sem=meta_recv.at[offset],
+            device_id=cell_id(offset),
+            device_id_type=MESH,
+        )
+        copy.start()
+        meta_copies.append(copy)
+
+    @pl.when(is_home)
+    def _():
+        left_out.start()
+
+    for chunk in range(chunks):
+        await_arrival(base, chunk, is_guest)
+        for way in ("up", "down", "partner"):
+            send(base, chunk, way, is_guest)
+
+    for step in range(1, col_count):
+        for chunk in range(chunks):
+            for origin, has, way in (
+                (c - step, c >= step, "up"),
+                (c + step, c + step < col_count, "down"),
+            ):
+                cell = k * col_count + jnp.clip(origin, 0, col_count - 1)
+                await_arrival(cell, chunk, has)
+                send(cell, chunk, way, has)
+                send(cell, chunk, "partner", has)
+
+    for chunk in range(chunks):
+        await_arrival((1 - k) * col_count + c, chunk, is_home)
+    for step in range(1, col_count):
+        cell = (1 - k) * col_count + lax.rem(c + step, col_count)
+        for chunk in range(chunks):
+            await_arrival(cell, chunk, True)
+
+    for copy in meta_copies:
+        copy.wait()
+    table_copy = pltpu.make_async_copy(meta_all, meta_smem, local_sem.at[3])
+    table_copy.start()
+    table_copy.wait()
+
+    @pl.when(is_home)
+    def _():
+        left_copy.wait()
+
+    @pl.when(is_guest)
+    def _():
+        left_out.wait_recv()
+
+    first = group * per_layer * slots
+
+    def one_row(i, carry):
+        block_row = base * n + i
+        targets = [meta_smem[block_row, 0, first + s] for s in range(per_layer * slots)]
+        strips = []
+        for a in range(width):
+            column = meta_smem[block_row, 0, a]
+            inner = jnp.maximum(column, 0)
+            pieces = []
+            for s in range(per_layer * slots):
+                part = s // slots
+                row_index = jnp.int32(cells * n)
+                slot_index = jnp.int32(0)
+                is_live = (column >= 0) & (targets[s] >= 0)
+                for t in range(slots):
+                    hit = (meta_smem[inner, 0, first + part * slots + t] == targets[s]) & is_live
+                    row_index = jnp.where(hit, inner, row_index)
+                    slot_index = jnp.where(hit, t, slot_index)
+                pieces.append(right[row_index, part, slot_index])
+            strips.append(jnp.concatenate(pieces, axis=1))
+        rights = jnp.concatenate(strips, axis=0)
+        lefts = jnp.concatenate(
+            [left[i, a // slots, a % slots] for a in range(width)], axis=1
+        )
+        total = jnp.dot(lefts, rights, preferred_element_type=jnp.float32).astype(stage.dtype)
+        for q in range(layer_count):
+            for s in range(per_layer * slots):
+                stage[q, i, s // slots, s % slots] = total[
+                    q * quarter:(q + 1) * quarter, s * tile:(s + 1) * tile
+                ]
+        return carry
+
+    out_rows = n // out_chunks
+
+    def out_copy(chunk, q, source):
+        rows = pl.ds(chunk * out_rows, out_rows)
+        return pltpu.make_async_remote_copy(
+            src_ref=stage.at[q, rows],
+            dst_ref=out_ref.at[rows, pl.ds(source * per_layer, per_layer)],
+            send_sem=out_send.at[q, chunk],
+            recv_sem=out_recv.at[source, chunk],
+            device_id={"row": k, "layer": q},
+            device_id_type=MESH,
+        )
+
+    def kept_copy(chunk):
+        rows = pl.ds(chunk * out_rows, out_rows)
+        return pltpu.make_async_copy(
+            stage.at[l, rows], out_ref.at[rows, own_groups], out_send.at[l, chunk]
+        )
+
+    for chunk in range(out_chunks + 1):
+        if chunk < out_chunks:
+            lax.fori_loop(chunk * out_rows, (chunk + 1) * out_rows, one_row, 0)
+        if chunk > 0:
+            for offset in range(layer_count - 1, -1, -1):
+                q = lax.rem(l + offset, layer_count)
+                if offset:
+                    out_copy(chunk - 1, q, group).start()
+                else:
+                    @pl.when(is_guest)
+                    def _():
+                        out_copy(chunk - 1, q, group).start()
+
+                    @pl.when(is_home)
+                    def _():
+                        kept_copy(chunk - 1).start()
+
+    for wanted, cell, chunk, index, device in sent:
+        @pl.when(wanted)
+        def _():
+            copy_of(cell, chunk, index, device).wait_send()
+
+    @pl.when(is_home)
+    def _():
+        left_out.wait_send()
+
+    for chunk in range(out_chunks):
+        for offset in range(layer_count):
+            q = lax.rem(l + offset, layer_count)
+            source = lax.rem(group + offset, layer_count)
+            if offset:
+                out_copy(chunk, q, source).wait()
+            else:
+                @pl.when(is_guest)
+                def _():
+                    out_copy(chunk, q, source).wait()
+
+                @pl.when(is_home)
+                def _():
+                    kept_copy(chunk).wait()
+
+
+def on_device_paired(density_tiles, tile_columns):
+    col_count = lax.axis_size("col")
+    layer_count = lax.axis_size("layer")
+    n, group_count, slots, tile, _ = density_tiles.shape
+    cells = 2 * col_count
+    per_layer = group_count // layer_count
+    quarter = tile // layer_count
+    width = group_count * slots
+    chunks = divisor(n, 4)
+    out_chunks = divisor(n, 8)
+    lanes = -(-width // 128) * 128
+    meta = jnp.pad(
+        tile_columns.reshape(n, 1, width), ((0, 0), (0, 0), (0, lanes - width)), constant_values=-1
+    )
+    dtype = density_tiles.dtype
+    return pl.pallas_call(
+        functools.partial(paired_kernel, (col_count, layer_count, chunks, out_chunks)),
+        out_shape=jax.ShapeDtypeStruct((n, group_count, slots, quarter, tile), dtype),
+        in_specs=[
+            pl.BlockSpec(memory_space=pl.ANY),
+            pl.BlockSpec(memory_space=pltpu.VMEM),
+        ],
+        out_specs=pl.BlockSpec(memory_space=pl.ANY),
+        scratch_shapes=[
+            pltpu.VMEM(density_tiles.shape, dtype),
+            pltpu.VMEM((cells * n + 1, per_layer, slots, tile, tile), dtype),
+            pltpu.VMEM((cells * n, 1, lanes), jnp.int32),
+            pltpu.SMEM((cells * n, 1, lanes), jnp.int32),
+            pltpu.VMEM((layer_count, n, per_layer, slots, quarter, tile), dtype),
+            pltpu.SemaphoreType.DMA((4,)),
+            pltpu.SemaphoreType.DMA((cells,)),
+            pltpu.SemaphoreType.DMA((cells,)),
+            pltpu.SemaphoreType.DMA((4, cells, chunks)),
+            pltpu.SemaphoreType.DMA((cells, chunks)),
+            pltpu.SemaphoreType.DMA,
+            pltpu.SemaphoreType.DMA,
+            pltpu.SemaphoreType.DMA((layer_count, out_chunks)),
+            pltpu.SemaphoreType.DMA((layer_count, out_chunks)),
+        ],
+        compiler_params=pltpu.CompilerParams(
+            collective_id=1, has_side_effects=True, vmem_limit_bytes=60 * 1024 * 1024
+        ),
+    )(density_tiles, meta)
+
+
 def solution(mesh):
+    paired = mesh.shape["row"] == 2 and mesh.shape["layer"] % 2 == 0
     in_specs = (P(("row", "col"), None, None, None, None), P(("row", "col"), None, None))
     out_specs = P(("row", "col"), None, None, "layer", None)
     return jax.shard_map(
-        on_device, mesh=mesh, in_specs=in_specs, out_specs=out_specs, check_vma=False
+        on_device_paired if paired else on_device, mesh=mesh, in_specs=in_specs, out_specs=out_specs, check_vma=False
     )

time: 158 us -> 141 us (0.89)
  Pallas kernels: 152 us -> 136 us
    pallas_call x1, Pallas kernels: 152 us -> 136 us  [on_device_paired(): pl.pallas_call(functools.partial(paired_kernel, (col_count, layer_count,...]
    unnamed x2 -> x1, local copies, waits for them, and re-layouts: 3.78 us -> 2.99 us
where the time goes in v2:
time: 141 us
  Pallas kernels  136 us (96%)
  local copies, waits for them, and re-layouts  4.35 us (3%)
    pallas_call x1, Pallas kernels, on_device_paired(): pl.pallas_call(functools.partial(paired_kernel, (col_count, layer_count,...  136 us
    unnamed x1, local copies, waits for them, and re-layouts  2.99 us

profile of v2, /device:TPU:0, one launch (start us, length us, event | category | flops | bytes accessed | tf_op | source)
XLA Modules:
  0.0 140.5 jit_solution(5447723522221900842)
XLA Ops:
  0.0 0.8 copy.4
  0.8 0.6 pad.4.meta_ref
  1.4 136.2 %shard_map.28 = bf16[24,4,2,32,128]{4,3,2,1,0:T(8,128)(2,1)} custom-call(bf16[24,4,2,128,128]{4,3,2,1,0:T(8,128)(2,1)} %tiles_ref.1, s32[24,1,128]{2,1,0:T(1,128)} %pad.4.meta_ref), custom_call_target="tpu_custom_call" | custom-call | tf_op jit(solution)/shard_map/pallas_call | solution.py:555
  137.5 3.0 %copy.6 = bf16[24,4,2,32,128]{4,3,2,1,0:T(8,128)(2,1)} copy(bf16[24,4,2,32,128]{4,3,2,1,0:T(8,128)(2,1)} %shard_map.28) | data formatting | bytes 3145728

commit v3 on v2

--- a/solution.py
+++ b/solution.py
@@ -545,8 +545,8 @@
     per_layer = group_count // layer_count
     quarter = tile // layer_count
     width = group_count * slots
-    chunks = divisor(n, 4)
-    out_chunks = divisor(n, 8)
+    chunks = divisor(n, 2)
+    out_chunks = divisor(n, 12)
     lanes = -(-width // 128) * 128
     meta = jnp.pad(
         tile_columns.reshape(n, 1, width), ((0, 0), (0, 0), (0, lanes - width)), constant_values=-1

time: 141 us -> 140 us (level)
  no operation moved by 1% of the time
where the time goes in v3:
time: 140 us; the launch traced here: 139 us
  Pallas kernels  135 us (96%)
  local copies, waits for them, and re-layouts  4.35 us (3%)
    pallas_call x1, Pallas kernels, on_device_paired(): pl.pallas_call(functools.partial(paired_kernel, (col_count, layer_count,...  135 us
    unnamed x1, local copies, waits for them, and re-layouts  2.99 us

profile of v3, /device:TPU:0, one launch (start us, length us, event | category | flops | bytes accessed | tf_op | source)
XLA Modules:
  0.0 139.5 jit_solution(11806707812941720561)
XLA Ops:
  0.0 0.8 copy.4
  0.8 0.6 pad.4.meta_ref
  1.4 135.1 %shard_map.28 = bf16[24,4,2,32,128]{4,3,2,1,0:T(8,128)(2,1)} custom-call(bf16[24,4,2,128,128]{4,3,2,1,0:T(8,128)(2,1)} %tiles_ref.1, s32[24,1,128]{2,1,0:T(1,128)} %pad.4.meta_ref), custom_call_target="tpu_custom_call" | custom-call | tf_op jit(solution)/shard_map/pallas_call | solution.py:555
  136.5 3.0 %copy.6 = bf16[24,4,2,32,128]{4,3,2,1,0:T(8,128)(2,1)} copy(bf16[24,4,2,32,128]{4,3,2,1,0:T(8,128)(2,1)} %shard_map.28) | data formatting | bytes 3145728
